TPU v7x, 32 devices: a whole 2x2x4 slice. The times are simulated.
32 devices in a mesh: cohort: 2 (over x), tile: 16 (over z, y, core).
Axes of the slice: x: 2, y: 2, z: 4, core: 2. Of those that a mesh axis runs over, the one named last changes fastest.
Arguments:
- dosage: bfloat16 [512, 8192], P(('cohort', 'tile')), parts along dimension 0, may hold values from 0 to 2
- covars: float32 [512, 16], P(('cohort', 'tile')), parts along dimension 0, may hold values from -12 to 12, as said below
- phenotypes: float32 [512, 1792], P(('cohort', 'tile')), parts along dimension 0, may hold values from -100 to 100
Outputs:
- mean_chi: float32 [3584], P(('cohort', 'tile')), parts along dimension 0
- hit_rate: float32 [3584], P(('cohort', 'tile')), parts along dimension 0
There are 2 independent parts, one for each index of `cohort`. A program takes and returns all parts, laid end to end along the dimension named above; each array names one. Nothing has to cross between parts.
Inputs may be any that keep to these rules, and one draw needn't show every extreme that they name: `covars`: each covariate column has its own mean and spread.
All inputs are finite; a program needn't handle non-finite values.
Results may differ from a plain program's by a relative error of at most 0.003.
Values may be sent and summed in bfloat16 or wider, within the bound.
A program may use at most 64 MiB of HBM per device.

v0:
```python
import jax
import jax.numpy as jnp
from jax import lax
from jax.sharding import PartitionSpec as P


def local(dosage, covars, phenotypes):
    highest = lax.Precision.HIGHEST
    devices = lax.axis_size("tile")
    local_rows = dosage.shape[0]
    variants = dosage.shape[1]
    samples = local_rows * devices
    genes_all = phenotypes.shape[1]
    gene_own = genes_all // devices
    scale_root = jnp.sqrt(jnp.float32(samples))
    covars_all = lax.all_gather(covars, "tile", axis=0, tiled=True)
    dose_all = lax.all_gather(dosage, "tile", axis=0, tiled=True)
    pheno_own = lax.all_to_all(phenotypes, "tile", split_axis=1, concat_axis=0, tiled=True)
    gram = jnp.dot(covars_all.T, covars_all, precision=highest, preferred_element_type=jnp.float32)
    factor = jnp.linalg.cholesky(gram)
    cov_pheno = jnp.dot(
        covars_all.T, pheno_own, precision=highest, preferred_element_type=jnp.float32
    )
    beta_pheno = jax.scipy.linalg.cho_solve((factor, True), cov_pheno)
    pheno_resid = pheno_own - jnp.dot(
        covars_all, beta_pheno, precision=highest, preferred_element_type=jnp.float32
    )
    pheno_sumsq = jnp.sum(pheno_resid * pheno_resid, axis=0)
    pheno_bf = pheno_resid.astype(jnp.bfloat16)
    pheno_var = pheno_sumsq / samples + 0.1
    width = 1024
    blocks = variants // width

    def one_block(index, totals):
        start = index * width
        dose_block = lax.dynamic_slice_in_dim(dose_all, start, width, 1).astype(jnp.float32)
        cov_dose = jnp.dot(
            covars_all.T, dose_block, precision=highest, preferred_element_type=jnp.float32
        )
        beta_dose = jax.scipy.linalg.cho_solve((factor, True), cov_dose)
        dose_resid = dose_block - jnp.dot(
            covars_all, beta_dose, precision=highest, preferred_element_type=jnp.float32
        )
        dose_var = jnp.sum(dose_resid * dose_resid, axis=0) / samples + 0.1
        cross = lax.dot_general(
            pheno_bf,
            dose_resid.astype(jnp.bfloat16),
            (((0,), (0,)), ((), ())),
            preferred_element_type=jnp.float32,
        )
        zscore = cross / (scale_root * jnp.sqrt(pheno_var[:, None] * dose_var[None, :]))
        chi_square = zscore * zscore
        return (
            totals[0] + jnp.sum(chi_square, axis=1),
            totals[1] + jnp.sum(jax.nn.sigmoid(2.0 * (chi_square - 4.0)), axis=1),
        )

    zeros = jnp.zeros((gene_own,), jnp.float32)
    chi_total, hit_total = lax.fori_loop(0, blocks, one_block, (zeros, zeros))
    return (chi_total / variants, 20.0 / variants * hit_total)


def solution(mesh):
    return jax.shard_map(
        local,
        mesh=mesh,
        in_specs=(
            P(("cohort", "tile"), None),
            P(("cohort", "tile"), None),
            P(("cohort", "tile"), None),
        ),
        out_specs=(P(("cohort", "tile")), P(("cohort", "tile"))),
        check_vma=False,
    )
```

profile of v0, /device:TPU:0, one launch (start us, length us, event | category | flops | bytes accessed | tf_op | source)
XLA Modules:
  0.0 117.5 jit_solution(11533161251048784845)
XLA Ops:
  7.2 0.7 all-gather.2.cloned.1.call-update
  7.9 1.0 all_to_all.14
  8.9 0.7 copy.15
  9.6 7.4 %all-to-all-start = ((f32[16,16,112]{2,0,1:T(8,128)}), f32[16,16,112]{2,0,1:T(8,128)S(1)}, u32[]{:S(2)}, u32[]{:S(2)}) async-start(f32[16,16,112]{2,0,1:T(8,128)} %copy.15), calls=%async_computation | async-start | bytes 262144 | tf_op jit(solution)/shard_map/all_to_all | solution.py:18
  17.0 22.7 %all_gather.7 = f32[256,16]{1,0:T(8,128)S(1)} all-gather(f32[16,16]{1,0:T(8,128)} %param.6), channel_id=1, replica_groups=mesh['cohort'=2,'tile'=16] {'tile'}, dimensions={0}, use_global_device_ids=true | all-gather | bytes 17408 | tf_op jit(solution)/shard_map/all_gather | solution.py:16
  39.8 0.4 fusion.20
  40.2 1.5 %cholesky.18 = f32[16,16]{1,0:T(8,128)S(1)} custom-call(f32[16,16]{1,0:T(8,128)S(1)} %fusion.19), custom_call_target="Cholesky" | custom-call | tf_op jit(solution)/shard_map/jit(cholesky)/cholesky | solution.py:20
  41.7 0.6 compare_reduce_fusion
  42.4 0.6 select_bitcast_fusion
  43.0 1.2 %custom-call.24 = f32[1,16,16]{1,2,0:T(8,128)S(1)} custom-call(f32[1,16,16]{2,1,0:T(8,128)S(1)} %get-tuple-element.272), custom_call_target="InvertDiagBlocksLowerTriangular" | custom-call | tf_op jit(solution)/shard_map/jit(_cho_solve)/triangular_solve | solution.py:24
  44.4 0.3 fusion.21
  45.1 0.4 multiply_reduce_fusion.1
  45.6 18.0 %all-gather.2.cloned.1.call-done = bf16[256,8192]{1,0:T(8,128)(2,1)} async-done(((bf16[16,8192]{1,0:T(8,128)(2,1)}), bf16[256,8192]{1,0:T(8,128)(2,1)}) %all-gather.2.cloned.1.call-update) | async-done | bytes 4194320 | tf_op jit(solution)/shard_map/all_gather | solution.py:17
  63.6 46.5 %while.18 = (s32[]{:T(128)}, f32[112]{0:T(128)S(1)}, f32[112]{0:T(128)S(1)}, bf16[256,8192]{1,0:T(8,128)(2,1)}, f32[16,16]{1,0:T(8,128)S(1)}, /*index=5*/f32[256...) while((s32[]{:T(128)}, f32[112]{0:T(128)S(1)}, ...), condition=%wide.region_7.8_spmd.clone, body=%wide.region_3.7_spmd.clone.sunk | while | flops 168249056 | bytes 2605173 | solution.py:59
  63.6 1.4 %fusion.62 = f32[1024,16]{0,1:T(8,128)S(1)} fusion(f32[256,16]{0,1:T(8,128)S(1)} %get-tuple-element.375, bf16[256,8192]{1,0:T(8,128)(2,1)} %get-tuple-element.373, s32[]{:T(128)S(6)} %select_n.19), kind=kOutput, calls=%fused_computation.7.clone.1 | convolution fusion | flops 50331648 | bytes 606212 | tf_op jit(solution)/shard_map/while/body/eval_jaxpr/dot_general | solution.py:37
  65.0 1.2 %custom-call.29 = f32[1,16,16]{1,2,0:T(8,128)S(1)} custom-call(f32[1,16,16]{2,1,0:T(8,128)S(1)} %bitcast_select_fusion.2), custom_call_target="InvertDiagBlocksLowerTriangular" | custom-call | tf_op jit(solution)/shard_map/while/body/eval_jaxpr/jit(_cho_solve)/triangular_solve | solution.py:40
  66.2 0.3 fusion.63
  66.7 2.1 %multiply_reduce_fusion.3 = (f32[1024]{0:T(1024)S(1)}, bf16[256,1024]{1,0:T(8,128)(2,1)S(1)}) fusion(f32[16,1024]{1,0:T(8,128)S(1)} %fusion.64, f32[256,16]{0,1:T(8,128)S(1)} %get-tuple-element.375, bf16[256,8192]{1,0:T(8,128)(2,1)} %get-tuple-element.373, s32[]{:T(128)S(6)} %select_n.19), kind=kOutput, calls=%fused_computation.5.clone.1 | convolution fusion | flops 51641344 | bytes 1134596 | tf_op jit(solution)/shard_map/while/body/eval_jaxpr/dot_general | solution.py:41
  68.8 0.6 fusion.65
  69.4 1.4 %fusion.62 = f32[1024,16]{0,1:T(8,128)S(1)} fusion(f32[256,16]{0,1:T(8,128)S(1)} %get-tuple-element.375, bf16[256,8192]{1,0:T(8,128)(2,1)} %get-tuple-element.373, s32[]{:T(128)S(6)} %select_n.19), kind=kOutput, calls=%fused_computation.7.clone.1 | convolution fusion | flops 50331648 | bytes 606212 | tf_op jit(solution)/shard_map/while/body/eval_jaxpr/dot_general | solution.py:37
  70.8 1.2 %custom-call.29 = f32[1,16,16]{1,2,0:T(8,128)S(1)} custom-call(f32[1,16,16]{2,1,0:T(8,128)S(1)} %bitcast_select_fusion.2), custom_call_target="InvertDiagBlocksLowerTriangular" | custom-call | tf_op jit(solution)/shard_map/while/body/eval_jaxpr/jit(_cho_solve)/triangular_solve | solution.py:40
  72.5 2.1 %multiply_reduce_fusion.3 = (f32[1024]{0:T(1024)S(1)}, bf16[256,1024]{1,0:T(8,128)(2,1)S(1)}) fusion(f32[16,1024]{1,0:T(8,128)S(1)} %fusion.64, f32[256,16]{0,1:T(8,128)S(1)} %get-tuple-element.375, bf16[256,8192]{1,0:T(8,128)(2,1)} %get-tuple-element.373, s32[]{:T(128)S(6)} %select_n.19), kind=kOutput, calls=%fused_computation.5.clone.1 | convolution fusion | flops 51641344 | bytes 1134596 | tf_op jit(solution)/shard_map/while/body/eval_jaxpr/dot_general | solution.py:41
  74.7 0.6 fusion.65
  75.2 1.4 %fusion.62 = f32[1024,16]{0,1:T(8,128)S(1)} fusion(f32[256,16]{0,1:T(8,128)S(1)} %get-tuple-element.375, bf16[256,8192]{1,0:T(8,128)(2,1)} %get-tuple-element.373, s32[]{:T(128)S(6)} %select_n.19), kind=kOutput, calls=%fused_computation.7.clone.1 | convolution fusion | flops 50331648 | bytes 606212 | tf_op jit(solution)/shard_map/while/body/eval_jaxpr/dot_general | solution.py:37
  76.6 1.2 %custom-call.29 = f32[1,16,16]{1,2,0:T(8,128)S(1)} custom-call(f32[1,16,16]{2,1,0:T(8,128)S(1)} %bitcast_select_fusion.2), custom_call_target="InvertDiagBlocksLowerTriangular" | custom-call | tf_op jit(solution)/shard_map/while/body/eval_jaxpr/jit(_cho_solve)/triangular_solve | solution.py:40
  78.3 2.1 %multiply_reduce_fusion.3 = (f32[1024]{0:T(1024)S(1)}, bf16[256,1024]{1,0:T(8,128)(2,1)S(1)}) fusion(f32[16,1024]{1,0:T(8,128)S(1)} %fusion.64, f32[256,16]{0,1:T(8,128)S(1)} %get-tuple-element.375, bf16[256,8192]{1,0:T(8,128)(2,1)} %get-tuple-element.373, s32[]{:T(128)S(6)} %select_n.19), kind=kOutput, calls=%fused_computation.5.clone.1 | convolution fusion | flops 51641344 | bytes 1134596 | tf_op jit(solution)/shard_map/while/body/eval_jaxpr/dot_general | solution.py:41
  80.5 0.6 fusion.65
  81.1 1.4 %fusion.62 = f32[1024,16]{0,1:T(8,128)S(1)} fusion(f32[256,16]{0,1:T(8,128)S(1)} %get-tuple-element.375, bf16[256,8192]{1,0:T(8,128)(2,1)} %get-tuple-element.373, s32[]{:T(128)S(6)} %select_n.19), kind=kOutput, calls=%fused_computation.7.clone.1 | convolution fusion | flops 50331648 | bytes 606212 | tf_op jit(solution)/shard_map/while/body/eval_jaxpr/dot_general | solution.py:37
  82.4 1.2 %custom-call.29 = f32[1,16,16]{1,2,0:T(8,128)S(1)} custom-call(f32[1,16,16]{2,1,0:T(8,128)S(1)} %bitcast_select_fusion.2), custom_call_target="InvertDiagBlocksLowerTriangular" | custom-call | tf_op jit(solution)/shard_map/while/body/eval_jaxpr/jit(_cho_solve)/triangular_solve | solution.py:40
  84.1 2.1 %multiply_reduce_fusion.3 = (f32[1024]{0:T(1024)S(1)}, bf16[256,1024]{1,0:T(8,128)(2,1)S(1)}) fusion(f32[16,1024]{1,0:T(8,128)S(1)} %fusion.64, f32[256,16]{0,1:T(8,128)S(1)} %get-tuple-element.375, bf16[256,8192]{1,0:T(8,128)(2,1)} %get-tuple-element.373, s32[]{:T(128)S(6)} %select_n.19), kind=kOutput, calls=%fused_computation.5.clone.1 | convolution fusion | flops 51641344 | bytes 1134596 | tf_op jit(solution)/shard_map/while/body/eval_jaxpr/dot_general | solution.py:41
  86.3 0.6 fusion.65
  86.9 1.4 %fusion.62 = f32[1024,16]{0,1:T(8,128)S(1)} fusion(f32[256,16]{0,1:T(8,128)S(1)} %get-tuple-element.375, bf16[256,8192]{1,0:T(8,128)(2,1)} %get-tuple-element.373, s32[]{:T(128)S(6)} %select_n.19), kind=kOutput, calls=%fused_computation.7.clone.1 | convolution fusion | flops 50331648 | bytes 606212 | tf_op jit(solution)/shard_map/while/body/eval_jaxpr/dot_general | solution.py:37
  88.2 1.2 %custom-call.29 = f32[1,16,16]{1,2,0:T(8,128)S(1)} custom-call(f32[1,16,16]{2,1,0:T(8,128)S(1)} %bitcast_select_fusion.2), custom_call_target="InvertDiagBlocksLowerTriangular" | custom-call | tf_op jit(solution)/shard_map/while/body/eval_jaxpr/jit(_cho_solve)/triangular_solve | solution.py:40
  90.0 2.1 %multiply_reduce_fusion.3 = (f32[1024]{0:T(1024)S(1)}, bf16[256,1024]{1,0:T(8,128)(2,1)S(1)}) fusion(f32[16,1024]{1,0:T(8,128)S(1)} %fusion.64, f32[256,16]{0,1:T(8,128)S(1)} %get-tuple-element.375, bf16[256,8192]{1,0:T(8,128)(2,1)} %get-tuple-element.373, s32[]{:T(128)S(6)} %select_n.19), kind=kOutput, calls=%fused_computation.5.clone.1 | convolution fusion | flops 51641344 | bytes 1134596 | tf_op jit(solution)/shard_map/while/body/eval_jaxpr/dot_general | solution.py:41
  92.1 0.6 fusion.65
  92.7 1.4 %fusion.62 = f32[1024,16]{0,1:T(8,128)S(1)} fusion(f32[256,16]{0,1:T(8,128)S(1)} %get-tuple-element.375, bf16[256,8192]{1,0:T(8,128)(2,1)} %get-tuple-element.373, s32[]{:T(128)S(6)} %select_n.19), kind=kOutput, calls=%fused_computation.7.clone.1 | convolution fusion | flops 50331648 | bytes 606212 | tf_op jit(solution)/shard_map/while/body/eval_jaxpr/dot_general | solution.py:37
  94.1 1.2 %custom-call.29 = f32[1,16,16]{1,2,0:T(8,128)S(1)} custom-call(f32[1,16,16]{2,1,0:T(8,128)S(1)} %bitcast_select_fusion.2), custom_call_target="InvertDiagBlocksLowerTriangular" | custom-call | tf_op jit(solution)/shard_map/while/body/eval_jaxpr/jit(_cho_solve)/triangular_solve | solution.py:40
  95.8 2.1 %multiply_reduce_fusion.3 = (f32[1024]{0:T(1024)S(1)}, bf16[256,1024]{1,0:T(8,128)(2,1)S(1)}) fusion(f32[16,1024]{1,0:T(8,128)S(1)} %fusion.64, f32[256,16]{0,1:T(8,128)S(1)} %get-tuple-element.375, bf16[256,8192]{1,0:T(8,128)(2,1)} %get-tuple-element.373, s32[]{:T(128)S(6)} %select_n.19), kind=kOutput, calls=%fused_computation.5.clone.1 | convolution fusion | flops 51641344 | bytes 1134596 | tf_op jit(solution)/shard_map/while/body/eval_jaxpr/dot_general | solution.py:41
  97.9 0.6 fusion.65
  98.5 1.4 %fusion.62 = f32[1024,16]{0,1:T(8,128)S(1)} fusion(f32[256,16]{0,1:T(8,128)S(1)} %get-tuple-element.375, bf16[256,8192]{1,0:T(8,128)(2,1)} %get-tuple-element.373, s32[]{:T(128)S(6)} %select_n.19), kind=kOutput, calls=%fused_computation.7.clone.1 | convolution fusion | flops 50331648 | bytes 606212 | tf_op jit(solution)/shard_map/while/body/eval_jaxpr/dot_general | solution.py:37
  99.9 1.2 %custom-call.29 = f32[1,16,16]{1,2,0:T(8,128)S(1)} custom-call(f32[1,16,16]{2,1,0:T(8,128)S(1)} %bitcast_select_fusion.2), custom_call_target="InvertDiagBlocksLowerTriangular" | custom-call | tf_op jit(solution)/shard_map/while/body/eval_jaxpr/jit(_cho_solve)/triangular_solve | solution.py:40
  101.6 2.1 %multiply_reduce_fusion.3 = (f32[1024]{0:T(1024)S(1)}, bf16[256,1024]{1,0:T(8,128)(2,1)S(1)}) fusion(f32[16,1024]{1,0:T(8,128)S(1)} %fusion.64, f32[256,16]{0,1:T(8,128)S(1)} %get-tuple-element.375, bf16[256,8192]{1,0:T(8,128)(2,1)} %get-tuple-element.373, s32[]{:T(128)S(6)} %select_n.19), kind=kOutput, calls=%fused_computation.5.clone.1 | convolution fusion | flops 51641344 | bytes 1134596 | tf_op jit(solution)/shard_map/while/body/eval_jaxpr/dot_general | solution.py:41
  103.7 0.6 fusion.65
  104.3 1.4 %fusion.62 = f32[1024,16]{0,1:T(8,128)S(1)} fusion(f32[256,16]{0,1:T(8,128)S(1)} %get-tuple-element.375, bf16[256,8192]{1,0:T(8,128)(2,1)} %get-tuple-element.373, s32[]{:T(128)S(6)} %select_n.19), kind=kOutput, calls=%fused_computation.7.clone.1 | convolution fusion | flops 50331648 | bytes 606212 | tf_op jit(solution)/shard_map/while/body/eval_jaxpr/dot_general | solution.py:37
  105.7 1.2 %custom-call.29 = f32[1,16,16]{1,2,0:T(8,128)S(1)} custom-call(f32[1,16,16]{2,1,0:T(8,128)S(1)} %bitcast_select_fusion.2), custom_call_target="InvertDiagBlocksLowerTriangular" | custom-call | tf_op jit(solution)/shard_map/while/body/eval_jaxpr/jit(_cho_solve)/triangular_solve | solution.py:40
  107.4 2.1 %multiply_reduce_fusion.3 = (f32[1024]{0:T(1024)S(1)}, bf16[256,1024]{1,0:T(8,128)(2,1)S(1)}) fusion(f32[16,1024]{1,0:T(8,128)S(1)} %fusion.64, f32[256,16]{0,1:T(8,128)S(1)} %get-tuple-element.375, bf16[256,8192]{1,0:T(8,128)(2,1)} %get-tuple-element.373, s32[]{:T(128)S(6)} %select_n.19), kind=kOutput, calls=%fused_computation.5.clone.1 | convolution fusion | flops 51641344 | bytes 1134596 | tf_op jit(solution)/shard_map/while/body/eval_jaxpr/dot_general | solution.py:41
  109.5 0.6 fusion.65
  110.1 0.5 broadcast_multiply_fusion
  (52 shorter events, 4.4 us)
Async XLA Ops:
  7.2 56.5 %all-gather.2.cloned.1.call-start = ((), (), s32[]{:S(2)}) async-start(), calls=%async_computation.1 | async-start | bytes 4456448 | tf_op jit(solution)/shard_map/all_gather | solution.py:17
  9.6 34.7 %all-to-all-start = ((f32[16,16,112]{2,0,1:T(8,128)}), f32[16,16,112]{2,0,1:T(8,128)S(1)}, u32[]{:S(2)}, u32[]{:S(2)}) async-start(f32[16,16,112]{2,0,1:T(8,128)} %copy.15), calls=%async_computation | async-start | bytes 262144 | tf_op jit(solution)/shard_map/all_to_all | solution.py:18
Sparse Core Ops, SparseCore 0:
  10.1 53.4 all-gather.1
where the time goes:
time: 118 us; the launch traced here: 117 us
  matrix products  37.4 us (32%)
  blocking collectives  22.7 us (19%)
  waiting for transfers between devices  18.7 us (16%)
  other arithmetic  14.6 us (12%)
  between operations  14.1 us (12%)
  starting transfers between devices  7.45 us (6%)
  local copies, waits for them, and re-layouts  2.05 us (2%)
    all_gather x1, blocking collectives, local(): covars_all = lax.all_gather(covars, 'tile', axis=0, tiled=True)  22.7 us
    all_gather x1, waiting for transfers between devices, local(): dose_all = lax.all_gather(dosage, 'tile', axis=0, tiled=True)  18 us
    dot_general x8, matrix products, one_block(): jnp.dot(covars_all, beta_dose, precision=highest, preferred_element_type=...  17 us
    dot_general x8, matrix products, one_block(): jnp.dot(covars_all.T, dose_block, precision=highest, preferred_element_ty...  10.9 us
    another operation x16, other arithmetic, one_block(): beta_dose = jax.scipy.linalg.cho_solve((factor, True), cov_dose)  9.88 us
    all_to_all x1, starting transfers between devices, local(): lax.all_to_all(phenotypes, 'tile', split_axis=1, concat_axis=0, tiled=True)  7.41 us
    dot_general x8, matrix products, one_block(): lax.dot_general(pheno_bf, dose_resid.astype(jnp.bfloat16), (((0,), (0,)),...  4.42 us
    another operation x16, matrix products, one_block(): beta_dose = jax.scipy.linalg.cho_solve((factor, True), cov_dose)  3.7 us
  transfers between devices with their start and end apart: 2, of which 1 were waited for; matrix products, arithmetic and copies ran while one was open for 6% of the time, Pallas kernels for 0%

commit v1 on v0

v1 whole, which is shorter than its diff:
```python
import functools

import jax
import jax.numpy as jnp
from jax import lax
from jax.experimental import pallas as pl
from jax.experimental.pallas import tpu as pltpu
from jax.sharding import PartitionSpec as P

LANES = 128
HIGH = lax.Precision.HIGHEST


def dot(a, b, ca, cb, precision=HIGH):
    return lax.dot_general(
        a, b, (((ca,), (cb,)), ((), ())), precision=precision, preferred_element_type=jnp.float32
    )


def inverse(gram):
    size = gram.shape[0]
    row_id = lax.broadcasted_iota(jnp.int32, (size, 2 * size), 0)
    eye = (
        lax.broadcasted_iota(jnp.int32, (size, size), 0)
        == lax.broadcasted_iota(jnp.int32, (size, size), 1)
    ).astype(jnp.float32)
    work = jnp.concatenate([gram, eye], axis=1)
    for k in range(size):
        row = work[k : k + 1, :] / work[k : k + 1, k : k + 1]
        work = jnp.where(row_id == k, row, work - work[:, k : k + 1] * row)
    return work[:, size:]


def kernel(
    n, zs, ys, cs, own,
    dose_ref, cov_ref, pheno_ref, out_ref,
    cov_all, raw, dose_all, blocks, doset, scale, part, landed,
    cov_send, cov_recv, raw_send, raw_recv, dose_send, dose_recv,
    z_send, y_send, c_send, blk_recv, part_send, part_recv,
):
    me = lax.axis_index("tile")
    rows, variants = dose_ref.shape
    covs = cov_ref.shape[1]
    genes = pheno_ref.shape[1]
    nb = genes // LANES
    width = variants // n
    samples = rows * n
    c = lax.rem(me, cs)
    y = lax.rem(me // cs, ys)
    z = me // (cs * ys)

    def index(zi, yi, ci):
        return (zi * ys + yi) * cs + ci

    def remote(src, dst, ssem, rsem, dev):
        return pltpu.make_async_remote_copy(
            src_ref=src, dst_ref=dst, send_sem=ssem, recv_sem=rsem,
            device_id={"tile": dev}, device_id_type=pl.DeviceIdType.MESH,
        )

    def row_slice(t):
        return pl.ds(pl.multiple_of(t * rows, rows), rows)

    def lane_slice(start, size):
        return pl.ds(pl.multiple_of(start, LANES), size)

    barrier = pltpu.get_barrier_semaphore()
    for k in range(1, n):
        pl.semaphore_signal(
            barrier, inc=1, device_id={"tile": lax.rem(me + k, n)},
            device_id_type=pl.DeviceIdType.MESH,
        )
    pl.semaphore_wait(barrier, n - 1)

    def cov_copy(src, dev):
        return remote(cov_ref, cov_all.at[row_slice(src), :], cov_send.at[dev], cov_recv.at[src], dev)

    def raw_copy(src, dev):
        return remote(
            pheno_ref.at[:, lane_slice(dev * LANES, LANES)],
            raw.at[row_slice(src), :], raw_send.at[dev], raw_recv.at[src], dev,
        )

    def dose_copy(src, dev):
        return remote(
            dose_ref.at[:, lane_slice(dev * width, width)],
            dose_all.at[row_slice(src), :], dose_send.at[dev], dose_recv.at[src], dev,
        )

    def others(body):
        @pl.loop(1, n)
        def _(k):
            body(lax.rem(me + k, n))

    def send_first(dev):
        cov_copy(me, dev).start()

        @pl.when(dev < nb)
        def _():
            raw_copy(me, dev).start()

    others(send_first)
    others(lambda dev: dose_copy(me, dev).start())

    cov_all[row_slice(me), :] = cov_ref[...]
    dose_all[row_slice(me), :] = dose_ref[:, lane_slice(me * width, width)]

    others(lambda src: cov_copy(src, me).wait_recv())
    cov = cov_all[...]
    eye = (
        lax.broadcasted_iota(jnp.int32, (covs, covs), 0)
        == lax.broadcasted_iota(jnp.int32, (covs, covs), 1)
    ).astype(jnp.float32)
    covt = dot(eye, cov, 1, 1)
    solve = dot(cov, inverse(dot(covt, cov, 1, 0)), 1, 0)

    def blk_z(o, dev):
        return remote(blocks.at[o], blocks.at[o], z_send.at[dev // (cs * ys)], blk_recv.at[o], dev)

    def blk_y(o, dev):
        return remote(blocks.at[o], blocks.at[o], y_send.at[o], blk_recv.at[o], dev)

    def blk_c(o, dev):
        return remote(blocks.at[o], blocks.at[o], c_send.at[o], blk_recv.at[o], dev)

    y_dev = index(z, lax.rem(y + 1, ys), c)
    c_dev = index(z, y, lax.rem(c + 1, cs))

    @pl.when(me < nb)
    def _():
        raw[row_slice(me), :] = pheno_ref[:, lane_slice(me * LANES, LANES)]
        others(lambda src: raw_copy(src, me).wait_recv())
        pheno = raw[...]
        resid = pheno - dot(solve, dot(covt, pheno, 1, 0), 1, 0)
        var = jnp.sum(resid * resid, axis=0, keepdims=True) / samples + 0.1
        inv = 1.0 / var
        hi = inv.astype(jnp.bfloat16)
        rest = inv - hi.astype(jnp.float32)
        mid = rest.astype(jnp.bfloat16)
        low = (rest - mid.astype(jnp.float32)).astype(jnp.bfloat16)
        line = lax.broadcasted_iota(jnp.int32, (16, LANES), 0)
        extra = jnp.where(
            line == 0, hi.astype(jnp.float32),
            jnp.where(line == 1, mid.astype(jnp.float32),
                      jnp.where(line == 2, low.astype(jnp.float32), 0.0)),
        )
        blocks[me, pl.ds(samples, 16), :] = extra.astype(jnp.bfloat16)
        blocks[me, pl.ds(0, samples), :] = resid.astype(jnp.bfloat16)
        for k in range(1, zs):
            blk_z(me, index(lax.rem(z + k, zs), y, c)).start()
        if ys > 1:
            blk_y(me, y_dev).start()
        if cs > 1:
            blk_c(me, c_dev).start()

    others(lambda src: dose_copy(src, me).wait_recv())
    dose = dose_all[...].astype(jnp.float32).T
    dose = dose - dot(dot(dose, cov, 1, 0), solve, 1, 1)
    doset[...] = dose.astype(jnp.bfloat16)
    dose_var = jnp.sum(dose * dose, axis=1, keepdims=True) / samples + 0.1
    scale[...] = jnp.broadcast_to(1.0 / (samples * dose_var), scale.shape)

    def compute(o):
        extra = blocks[o, pl.ds(samples, 16), :].astype(jnp.float32)
        gene_scale = jnp.sum(extra[0:3, :], axis=0, keepdims=True)
        cross = dot(doset[...], blocks[o, pl.ds(0, samples), :], 1, 0, None)
        chi = cross * cross * (scale[...] * gene_scale)
        hit = 1.0 / (1.0 + jnp.exp(-2.0 * (chi - 4.0)))
        cols = lane_slice(o * LANES, LANES)
        part[0:1, cols] = jnp.sum(chi, axis=0, keepdims=True)
        part[1:2, cols] = jnp.sum(hit, axis=0, keepdims=True)

    @pl.when(me < nb)
    def _():
        compute(me)

    @pl.loop(1, zs)
    def _(k):
        o = index(lax.rem(z + k, zs), y, c)

        @pl.when(o < nb)
        def _():
            blk_z(o, me).wait_recv()
            if ys > 1:
                blk_y(o, y_dev).start()
            if cs > 1:
                blk_c(o, c_dev).start()
            compute(o)

    if ys > 1:
        @pl.loop(0, zs)
        def _(k):
            o = index(lax.rem(z + k, zs), lax.rem(y + 1, ys), c)

            @pl.when(o < nb)
            def _():
                blk_y(o, me).wait_recv()
                if cs > 1:
                    blk_c(o, c_dev).start()
                compute(o)

    if cs > 1:
        for j in range(ys):
            @pl.loop(0, zs)
            def _(k):
                o = index(lax.rem(z + k, zs), lax.rem(y + j, ys), lax.rem(c + 1, cs))

                @pl.when(o < nb)
                def _():
                    blk_c(o, me).wait_recv()
                    compute(o)

    window = landed.shape[2]

    def first(dev):
        return jnp.minimum(own * dev // LANES * LANES, genes - window)

    def part_copy(src, dev):
        return remote(
            part.at[:, lane_slice(first(dev), window)], landed.at[src],
            part_send.at[dev], part_recv.at[src], dev,
        )

    others(lambda dev: part_copy(me, dev).start())
    landed[me] = part[:, lane_slice(first(me), window)]
    others(lambda src: part_copy(src, me).wait_recv())
    total = jnp.sum(landed[...], axis=0)
    shift = own * me - first(me)
    out_ref[...] = pltpu.roll(total, lax.rem(window - shift, window), 1)

    def drain(dev):
        cov_copy(me, dev).wait_send()
        dose_copy(me, dev).wait_send()
        part_copy(me, dev).wait_send()

        @pl.when(dev < nb)
        def _():
            raw_copy(me, dev).wait_send()

    others(drain)

    @pl.when(me < nb)
    def _():
        for k in range(1, zs):
            blk_z(me, index(lax.rem(z + k, zs), y, c)).wait_send()

    @pl.loop(0, zs)
    def _(k):
        o = index(lax.rem(z + k, zs), y, c)

        @pl.when(o < nb)
        def _():
            if ys > 1:
                blk_y(o, y_dev).wait_send()
            if cs > 1:
                blk_c(o, c_dev).wait_send()

        if ys > 1 and cs > 1:
            other = index(lax.rem(z + k, zs), lax.rem(y + 1, ys), c)

            @pl.when(other < nb)
            def _():
                blk_c(other, c_dev).wait_send()


def local(dosage, covars, phenotypes):
    n = lax.axis_size("tile")
    rows, variants = dosage.shape
    genes = phenotypes.shape[1]
    covs = covars.shape[1]
    samples = rows * n
    cs = 2 if n % 2 == 0 else 1
    ys = 2 if n % (2 * cs) == 0 else 1
    zs = n // (cs * ys)
    nb = genes // LANES
    own = genes // n
    width = variants // n
    window = (own + LANES - 1 + LANES - 1) // LANES * LANES
    dma = pltpu.SemaphoreType.DMA
    out = pl.pallas_call(
        functools.partial(kernel, n, zs, ys, cs, own),
        out_shape=jax.ShapeDtypeStruct((8, window), jnp.float32),
        in_specs=[pl.BlockSpec(memory_space=pltpu.VMEM)] * 3,
        out_specs=pl.BlockSpec(memory_space=pltpu.VMEM),
        scratch_shapes=[
            pltpu.VMEM((samples, covs), jnp.float32),
            pltpu.VMEM((samples, LANES), jnp.float32),
            pltpu.VMEM((samples, width), jnp.bfloat16),
            pltpu.VMEM((nb, samples + 16, LANES), jnp.bfloat16),
            pltpu.VMEM((width, samples), jnp.bfloat16),
            pltpu.VMEM((width, LANES), jnp.float32),
            pltpu.VMEM((8, genes), jnp.float32),
            pltpu.VMEM((n, 8, window), jnp.float32),
            dma((n,)), dma((n,)), dma((n,)), dma((n,)), dma((n,)), dma((n,)),
            dma((zs,)), dma((nb,)), dma((nb,)), dma((nb,)), dma((n,)), dma((n,)),
        ],
        compiler_params=pltpu.CompilerParams(collective_id=0, has_side_effects=True),
    )(dosage, covars, phenotypes)
    return out[0, :own] / variants, 20.0 / variants * out[1, :own]


def solution(mesh):
    spec = P(("cohort", "tile"), None)
    return jax.shard_map(
        local,
        mesh=mesh,
        in_specs=(spec, spec, spec),
        out_specs=(P(("cohort", "tile")), P(("cohort", "tile"))),
        check_vma=False,
    )
```

time: 118 us -> 42.1 us (0.36)
  Pallas kernels: 0 us -> 40 us
  matrix products: 37.4 us -> 0 us
  blocking collectives: 22.7 us -> 0 us
  waiting for transfers between devices: 18.7 us -> 0 us
  between operations: 14.1 us -> 0.64 us
  other arithmetic: 14.6 us -> 1.27 us
  starting transfers between devices: 7.45 us -> 0 us
  local copies, waits for them, and re-layouts: 2.05 us -> 0 us
    pallas_call x0 -> x1, Pallas kernels: none -> 40 us  [local(): pl.pallas_call(functools.partial(kernel, n, zs, ys, cs, own), out_shape=j...]
    dot_general x27 -> x0, matrix products: 33.4 us -> none  [the longest x8 17 us: one_block(): jnp.dot(covars_all, beta_dose, precision=highest, preferred_element_type=...]
    all_gather x1 -> x0, blocking collectives: 22.7 us -> none  [local(): covars_all = lax.all_gather(covars, 'tile', axis=0, tiled=True)]
    all_gather x1 -> x0, waiting for transfers between devices: 18 us -> none  [local(): dose_all = lax.all_gather(dosage, 'tile', axis=0, tiled=True)]
    another operation x21 -> x0, other arithmetic: 13.9 us -> none  [the longest x16 9.88 us: one_block(): beta_dose = jax.scipy.linalg.cho_solve((factor, True), cov_dose)]
    all_to_all x1 -> x0, starting transfers between devices: 7.41 us -> none  [local(): lax.all_to_all(phenotypes, 'tile', split_axis=1, concat_axis=0, tiled=True)]
    another operation x18 -> x0, matrix products: 4.04 us -> none  [the longest x16 3.7 us: one_block(): beta_dose = jax.scipy.linalg.cho_solve((factor, True), cov_dose)]
    all_to_all x3 -> x0, local copies, waits for them, and re-layouts: 1.8 us -> none  [local(): lax.all_to_all(phenotypes, 'tile', split_axis=1, concat_axis=0, tiled=True)]
  transfers between devices with their start and end apart: 2 -> 0, of which waited for: 1 -> 0; matrix products, arithmetic and copies ran while one was open for 6% -> 0% of each run, Pallas kernels for 0% -> 0%
where the time goes in v1:
time: 42.1 us; the launch traced here: 41.9 us
  Pallas kernels  40 us (95%)
  other arithmetic  1.27 us (3%)
  between operations  0.64 us (2%)
    pallas_call x1, Pallas kernels, local(): pl.pallas_call(functools.partial(kernel, n, zs, ys, cs, own), out_shape=j...  40 us
    mul x1, other arithmetic, local(): return (out[0, :own] / variants, 20.0 / variants * out[1, :own])  1.27 us

profile of v1, /device:TPU:0, one launch (start us, length us, event | category | flops | bytes accessed | tf_op | source)
XLA Modules:
  0.0 41.9 jit_solution(6092334735880502933)
XLA Ops:
  0.6 40.0 %shard_map.50 = f32[8,256]{1,0:T(8,128)} custom-call(bf16[16,8192]{1,0:T(8,128)(2,1)} %dose_ref.1, f32[16,16]{1,0:T(8,128)} %cov_ref.1, f32[16,1792]{1,0:T(8,128)} %pheno_ref.1), custom_call_target="tpu_custom_call" | custom-call | tf_op jit(solution)/shard_map/pallas_call | solution.py:280
  40.6 1.3 %multiply_bitcast_fusion = (f32[112]{0:T(128)}, f32[112]{0:T(128)}) fusion(f32[8,256]{1,0:T(8,128)} %shard_map.50), kind=kLoop, calls=%fused_computation | loop fusion | flops 224 | bytes 1792 | tf_op jit(solution)/shard_map/mul | solution.py:299

commit v2 on v1

--- a/solution.py
+++ b/solution.py
@@ -35,7 +35,7 @@
     n, zs, ys, cs, own,
     dose_ref, cov_ref, pheno_ref, out_ref,
     cov_all, raw, dose_all, blocks, doset, scale, part, landed,
-    cov_send, cov_recv, raw_send, raw_recv, dose_send, dose_recv,
+    cov_own, cov_send, cov_recv, raw_send, raw_recv, dose_send, dose_recv,
     z_send, y_send, c_send, blk_recv, part_send, part_recv,
 ):
     me = lax.axis_index("tile")
@@ -64,6 +64,11 @@
     def lane_slice(start, size):
         return pl.ds(pl.multiple_of(start, LANES), size)
 
+    groups = rows // 8
+    packed = [cov_ref[8 * g : 8 * g + 8, :] for g in range(groups)]
+    fill = jnp.zeros((8, LANES - groups * covs), jnp.float32)
+    cov_own[...] = jnp.concatenate(packed + [fill], axis=1)
+
     barrier = pltpu.get_barrier_semaphore()
     for k in range(1, n):
         pl.semaphore_signal(
@@ -73,7 +78,7 @@
     pl.semaphore_wait(barrier, n - 1)
 
     def cov_copy(src, dev):
-        return remote(cov_ref, cov_all.at[row_slice(src), :], cov_send.at[dev], cov_recv.at[src], dev)
+        return remote(cov_own, cov_all.at[src], cov_send.at[dev], cov_recv.at[src], dev)
 
     def raw_copy(src, dev):
         return remote(
@@ -92,9 +97,9 @@
         def _(k):
             body(lax.rem(me + k, n))
 
+    others(lambda dev: cov_copy(me, dev).start())
+
     def send_first(dev):
-        cov_copy(me, dev).start()
-
         @pl.when(dev < nb)
         def _():
             raw_copy(me, dev).start()
@@ -102,11 +107,14 @@
     others(send_first)
     others(lambda dev: dose_copy(me, dev).start())
 
-    cov_all[row_slice(me), :] = cov_ref[...]
+    cov_all[me] = cov_own[...]
     dose_all[row_slice(me), :] = dose_ref[:, lane_slice(me * width, width)]
 
     others(lambda src: cov_copy(src, me).wait_recv())
-    cov = cov_all[...]
+    tiles = cov_all[...]
+    cov = jnp.concatenate(
+        [tiles[:, :, g * covs : (g + 1) * covs] for g in range(groups)], axis=1
+    ).reshape(samples, covs)
     eye = (
         lax.broadcasted_iota(jnp.int32, (covs, covs), 0)
         == lax.broadcasted_iota(jnp.int32, (covs, covs), 1)
@@ -283,7 +291,7 @@
         in_specs=[pl.BlockSpec(memory_space=pltpu.VMEM)] * 3,
         out_specs=pl.BlockSpec(memory_space=pltpu.VMEM),
         scratch_shapes=[
-            pltpu.VMEM((samples, covs), jnp.float32),
+            pltpu.VMEM((n, 8, LANES), jnp.float32),
             pltpu.VMEM((samples, LANES), jnp.float32),
             pltpu.VMEM((samples, width), jnp.bfloat16),
             pltpu.VMEM((nb, samples + 16, LANES), jnp.bfloat16),
@@ -291,6 +299,7 @@
             pltpu.VMEM((width, LANES), jnp.float32),
             pltpu.VMEM((8, genes), jnp.float32),
             pltpu.VMEM((n, 8, window), jnp.float32),
+            pltpu.VMEM((8, LANES), jnp.float32),
             dma((n,)), dma((n,)), dma((n,)), dma((n,)), dma((n,)), dma((n,)),
             dma((zs,)), dma((nb,)), dma((nb,)), dma((nb,)), dma((n,)), dma((n,)),
         ],

time: 42.1 us -> 40.8 us (0.969)
  Pallas kernels: 40 us -> 38.7 us
    pallas_call x1, Pallas kernels: 40 us -> 38.7 us  [local(): pl.pallas_call(functools.partial(kernel, n, zs, ys, cs, own), out_shape=j...]
where the time goes in v2:
time: 40.8 us; the launch traced here: 40.6 us
  Pallas kernels  38.7 us (95%)
  other arithmetic  1.27 us (3%)
  between operations  0.64 us (2%)
    pallas_call x1, Pallas kernels, local(): pl.pallas_call(functools.partial(kernel, n, zs, ys, cs, own), out_shape=j...  38.7 us
    mul x1, other arithmetic, local(): return (out[0, :own] / variants, 20.0 / variants * out[1, :own])  1.27 us

profile of v2, /device:TPU:0, one launch (start us, length us, event | category | flops | bytes accessed | tf_op | source)
XLA Modules:
  0.0 40.6 jit_solution(11286966614552979121)
XLA Ops:
  0.6 38.7 %shard_map.50 = f32[8,256]{1,0:T(8,128)} custom-call(bf16[16,8192]{1,0:T(8,128)(2,1)} %dose_ref.1, f32[16,16]{1,0:T(8,128)} %cov_ref.1, f32[16,1792]{1,0:T(8,128)} %pheno_ref.1), custom_call_target="tpu_custom_call" | custom-call | tf_op jit(solution)/shard_map/pallas_call | solution.py:288
  39.3 1.3 %multiply_bitcast_fusion = (f32[112]{0:T(128)}, f32[112]{0:T(128)}) fusion(f32[8,256]{1,0:T(8,128)} %shard_map.50), kind=kLoop, calls=%fused_computation | loop fusion | flops 224 | bytes 1792 | tf_op jit(solution)/shard_map/mul | solution.py:308

commit v3 on v2

v3 whole, which is shorter than its diff:
```python
import functools

import jax
import jax.numpy as jnp
from jax import lax
from jax.experimental import pallas as pl
from jax.experimental.pallas import tpu as pltpu
from jax.sharding import PartitionSpec as P

LANES = 128
HIGH = lax.Precision.HIGHEST


def dot(a, b, ca, cb, precision=HIGH):
    return lax.dot_general(
        a, b, (((ca,), (cb,)), ((), ())), precision=precision, preferred_element_type=jnp.float32
    )


def inverse(gram):
    size = gram.shape[0]
    row_id = lax.broadcasted_iota(jnp.int32, (size, 2 * size), 0)
    eye = (
        lax.broadcasted_iota(jnp.int32, (size, size), 0)
        == lax.broadcasted_iota(jnp.int32, (size, size), 1)
    ).astype(jnp.float32)
    work = jnp.concatenate([gram, eye], axis=1)
    for k in range(size):
        row = work[k : k + 1, :] / work[k : k + 1, k : k + 1]
        work = jnp.where(row_id == k, row, work - work[:, k : k + 1] * row)
    return work[:, size:]


def kernel(
    n, zs, ys, cs, own,
    dose_in, cov_in, pheno_in, out_ref,
    dose_ref, cov_ref, pheno_ref, load_sem,
    cov_all, raw, dose_all, blocks, doset, scale, part, landed,
    cov_own, cov_send, cov_recv, raw_send, raw_recv, dose_send, dose_recv,
    z_send, pass_send, c_send, blk_recv, part_send, part_recv,
):
    me = lax.axis_index("tile")
    rows, variants = dose_ref.shape
    covs = cov_ref.shape[1]
    genes = pheno_ref.shape[1]
    nb = genes // (ys * LANES)
    peers = zs * cs
    width = variants // peers
    samples = rows * n
    c = lax.rem(me, cs)
    y = lax.rem(me // cs, ys)
    z = me // (cs * ys)
    place = z * cs + c

    def index(zi, yi, ci):
        return (zi * ys + yi) * cs + ci

    def place_of(t):
        return t // (cs * ys) * cs + lax.rem(t, cs)

    def at_place(p):
        return index(p // cs, y, lax.rem(p, cs))

    def remote(src, dst, ssem, rsem, dev):
        return pltpu.make_async_remote_copy(
            src_ref=src, dst_ref=dst, send_sem=ssem, recv_sem=rsem,
            device_id={"tile": dev}, device_id_type=pl.DeviceIdType.MESH,
        )

    def row_slice(t):
        return pl.ds(pl.multiple_of(t * rows, rows), rows)

    def lane_slice(start, size):
        return pl.ds(pl.multiple_of(start, LANES), size)

    cov_load = pltpu.make_async_copy(cov_in, cov_ref, load_sem.at[0])
    pheno_load = pltpu.make_async_copy(pheno_in, pheno_ref, load_sem.at[1])
    dose_load = pltpu.make_async_copy(dose_in, dose_ref, load_sem.at[2])
    barrier = pltpu.get_barrier_semaphore()
    for k in range(1, n):
        pl.semaphore_signal(
            barrier, inc=1, device_id={"tile": lax.rem(me + k, n)},
            device_id_type=pl.DeviceIdType.MESH,
        )
    cov_load.start()
    pheno_load.start()
    dose_load.start()
    cov_load.wait()
    groups = rows // 8
    packed = [cov_ref[8 * g : 8 * g + 8, :] for g in range(groups)]
    fill = jnp.zeros((8, LANES - groups * covs), jnp.float32)
    cov_own[...] = jnp.concatenate(packed + [fill], axis=1)
    pheno_load.wait()
    dose_load.wait()
    pl.semaphore_wait(barrier, n - 1)

    def cov_copy(src, dev):
        return remote(cov_own, cov_all.at[src], cov_send.at[dev], cov_recv.at[src], dev)

    def raw_copy(src, dev):
        return remote(
            pheno_ref.at[:, lane_slice((lax.rem(dev // cs, ys) * nb + place_of(dev)) * LANES, LANES)],
            raw.at[row_slice(src), :], raw_send.at[dev], raw_recv.at[src], dev,
        )

    def dose_copy(src, dev):
        return remote(
            dose_ref.at[:, lane_slice(place_of(dev) * width, width)],
            dose_all.at[row_slice(src), :], dose_send.at[dev], dose_recv.at[src], dev,
        )

    def others(body):
        @pl.loop(1, n)
        def _(k):
            body(lax.rem(me + k, n))

    others(lambda dev: cov_copy(me, dev).start())

    def send_first(dev):
        @pl.when(place_of(dev) < nb)
        def _():
            raw_copy(me, dev).start()

    def group(body):
        @pl.loop(1, peers)
        def _(k):
            body(at_place(lax.rem(place + k, peers)))

    y_dev = index(z, lax.rem(y + 1, ys), c)
    c_dev = index(z, y, lax.rem(c + 1, cs))

    def dose_pass(src):
        return remote(
            dose_all.at[row_slice(src), :], dose_all.at[row_slice(src), :],
            pass_send.at[src], dose_recv.at[src], y_dev,
        )

    others(send_first)
    group(lambda dev: dose_copy(me, dev).start())
    if ys > 1:
        dose_copy(me, y_dev).start()

    cov_all[me] = cov_own[...]
    dose_all[row_slice(me), :] = dose_ref[:, lane_slice(place * width, width)]

    others(lambda src: cov_copy(src, me).wait_recv())
    tiles = cov_all[...]
    cov = jnp.concatenate(
        [tiles[:, :, g * covs : (g + 1) * covs] for g in range(groups)], axis=1
    ).reshape(samples, covs)
    eye = (
        lax.broadcasted_iota(jnp.int32, (covs, covs), 0)
        == lax.broadcasted_iota(jnp.int32, (covs, covs), 1)
    ).astype(jnp.float32)
    covt = dot(eye, cov, 1, 1)
    solve = dot(cov, inverse(dot(covt, cov, 1, 0)), 1, 0)

    def blk_z(o, dev):
        return remote(blocks.at[o], blocks.at[o], z_send.at[dev // (cs * ys)], blk_recv.at[o], dev)

    def blk_c(o, dev):
        return remote(blocks.at[o], blocks.at[o], c_send.at[o], blk_recv.at[o], dev)

    @pl.when(place < nb)
    def _():
        raw[row_slice(me), :] = pheno_ref[:, lane_slice((y * nb + place) * LANES, LANES)]
        others(lambda src: raw_copy(src, me).wait_recv())
        pheno = raw[...]
        resid = pheno - dot(solve, dot(covt, pheno, 1, 0), 1, 0)
        var = jnp.sum(resid * resid, axis=0, keepdims=True) / samples + 0.1
        inv = 1.0 / var
        hi = inv.astype(jnp.bfloat16)
        rest = inv - hi.astype(jnp.float32)
        mid = rest.astype(jnp.bfloat16)
        low = (rest - mid.astype(jnp.float32)).astype(jnp.bfloat16)
        line = lax.broadcasted_iota(jnp.int32, (16, LANES), 0)
        extra = jnp.where(
            line == 0, hi.astype(jnp.float32),
            jnp.where(line == 1, mid.astype(jnp.float32),
                      jnp.where(line == 2, low.astype(jnp.float32), 0.0)),
        )
        blocks[place, pl.ds(samples, 16), :] = extra.astype(jnp.bfloat16)
        blocks[place, pl.ds(0, samples), :] = resid.astype(jnp.bfloat16)
        for k in range(1, zs):
            blk_z(place, index(lax.rem(z + k, zs), y, c)).start()
        if cs > 1:
            blk_c(place, c_dev).start()

    def hand_on(src):
        dose_copy(src, me).wait_recv()
        if ys > 1:
            dose_pass(src).start()

    group(hand_on)
    if ys > 1:
        @pl.loop(0, peers)
        def _(k):
            p = lax.rem(place + k, peers)
            src = index(p // cs, lax.rem(y + 1, ys), lax.rem(p, cs))
            dose_copy(src, me).wait_recv()

    dose = dose_all[...].astype(jnp.float32).T
    dose = dose - dot(dot(dose, cov, 1, 0), solve, 1, 1)
    doset[...] = dose.astype(jnp.bfloat16)
    dose_var = jnp.sum(dose * dose, axis=1, keepdims=True) / samples + 0.1
    scale[...] = jnp.broadcast_to(1.0 / (samples * dose_var), scale.shape)

    def compute(o):
        extra = blocks[o, pl.ds(samples, 16), :].astype(jnp.float32)
        gene_scale = jnp.sum(extra[0:3, :], axis=0, keepdims=True)
        cross = dot(doset[...], blocks[o, pl.ds(0, samples), :], 1, 0, None)
        chi = cross * cross * (scale[...] * gene_scale)
        hit = 1.0 / (1.0 + jnp.exp(-2.0 * (chi - 4.0)))
        cols = lane_slice(o * LANES, LANES)
        part[0:1, cols] = jnp.sum(chi, axis=0, keepdims=True)
        part[1:2, cols] = jnp.sum(hit, axis=0, keepdims=True)

    @pl.when(place < nb)
    def _():
        compute(place)

    @pl.loop(1, zs)
    def _(k):
        o = lax.rem(z + k, zs) * cs + c

        @pl.when(o < nb)
        def _():
            blk_z(o, me).wait_recv()
            if cs > 1:
                blk_c(o, c_dev).start()
            compute(o)

    if cs > 1:
        @pl.loop(0, zs)
        def _(k):
            o = lax.rem(z + k, zs) * cs + lax.rem(c + 1, cs)

            @pl.when(o < nb)
            def _():
                blk_c(o, me).wait_recv()
                compute(o)

    window = landed.shape[2]

    def owner(k):
        return y * peers + lax.rem(place + k, peers)

    def first(dev):
        return jnp.minimum(own * lax.rem(dev, peers) // LANES * LANES, nb * LANES - window)

    def part_copy(src, dev):
        return remote(
            part.at[:, lane_slice(first(dev), window)], landed.at[place_of(src)],
            part_send.at[lax.rem(dev, peers)], part_recv.at[place_of(src)], dev,
        )

    def each_part(body):
        @pl.loop(0, peers)
        def _(k):
            dev = owner(k)

            @pl.when(dev != me)
            def _():
                body(dev)

    def each_source(body):
        @pl.loop(0, peers)
        def _(k):
            src = index(k // cs, me // peers, lax.rem(k, cs))

            @pl.when(src != me)
            def _():
                body(src)

    each_part(lambda dev: part_copy(me, dev).start())

    @pl.when(me // peers == y)
    def _():
        landed[place] = part[:, lane_slice(first(me), window)]

    each_source(lambda src: part_copy(src, me).wait_recv())
    total = jnp.sum(landed[...], axis=0)
    shift = own * lax.rem(me, peers) - first(me)
    out_ref[...] = pltpu.roll(total, lax.rem(window - shift, window), 1)

    def drain(dev):
        cov_copy(me, dev).wait_send()

        @pl.when(place_of(dev) < nb)
        def _():
            raw_copy(me, dev).wait_send()

    others(drain)

    def drain_dose(dev):
        dose_copy(me, dev).wait_send()
        if ys > 1:
            dose_pass(dev).wait_send()

    group(drain_dose)
    if ys > 1:
        dose_copy(me, y_dev).wait_send()
    each_part(lambda dev: part_copy(me, dev).wait_send())

    @pl.when(place < nb)
    def _():
        for k in range(1, zs):
            blk_z(place, index(lax.rem(z + k, zs), y, c)).wait_send()

    if cs > 1:
        @pl.loop(0, zs)
        def _(k):
            o = lax.rem(z + k, zs) * cs + c

            @pl.when(o < nb)
            def _():
                blk_c(o, c_dev).wait_send()


def local(dosage, covars, phenotypes):
    n = lax.axis_size("tile")
    rows, variants = dosage.shape
    genes = phenotypes.shape[1]
    covs = covars.shape[1]
    samples = rows * n
    cs = 2 if n % 2 == 0 else 1
    ys = 2 if n % (2 * cs) == 0 else 1
    zs = n // (cs * ys)
    peers = zs * cs
    nb = genes // (ys * LANES)
    own = genes // n
    width = variants // peers
    window = (own + LANES - 1 + LANES - 1) // LANES * LANES
    dma = pltpu.SemaphoreType.DMA
    out = pl.pallas_call(
        functools.partial(kernel, n, zs, ys, cs, own),
        out_shape=jax.ShapeDtypeStruct((8, window), jnp.float32),
        in_specs=[pl.BlockSpec(memory_space=pl.ANY)] * 3,
        out_specs=pl.BlockSpec(memory_space=pltpu.VMEM),
        scratch_shapes=[
            pltpu.VMEM(dosage.shape, dosage.dtype),
            pltpu.VMEM(covars.shape, covars.dtype),
            pltpu.VMEM(phenotypes.shape, phenotypes.dtype),
            dma((3,)),
            pltpu.VMEM((n, 8, LANES), jnp.float32),
            pltpu.VMEM((samples, LANES), jnp.float32),
            pltpu.VMEM((samples, width), jnp.bfloat16),
            pltpu.VMEM((nb, samples + 16, LANES), jnp.bfloat16),
            pltpu.VMEM((width, samples), jnp.bfloat16),
            pltpu.VMEM((width, LANES), jnp.float32),
            pltpu.VMEM((8, nb * LANES), jnp.float32),
            pltpu.VMEM((peers, 8, window), jnp.float32),
            pltpu.VMEM((8, LANES), jnp.float32),
            dma((n,)), dma((n,)), dma((n,)), dma((n,)), dma((n,)), dma((n,)),
            dma((zs,)), dma((n,)), dma((nb,)), dma((nb,)), dma((peers,)), dma((peers,)),
        ],
        compiler_params=pltpu.CompilerParams(collective_id=0, has_side_effects=True),
    )(dosage, covars, phenotypes)
    return out[0, :own] / variants, 20.0 / variants * out[1, :own]


def solution(mesh):
    spec = P(("cohort", "tile"), None)
    return jax.shard_map(
        local,
        mesh=mesh,
        in_specs=(spec, spec, spec),
        out_specs=(P(("cohort", "tile")), P(("cohort", "tile"))),
        check_vma=False,
    )
```

time: 40.8 us -> 37.1 us (0.909)
  Pallas kernels: 38.7 us -> 34.7 us
    pallas_call x1, Pallas kernels: 38.7 us -> 34.7 us  [local(): pl.pallas_call(functools.partial(kernel, n, zs, ys, cs, own), out_shape=j...]
where the time goes in v3:
time: 37.1 us; the launch traced here: 36.6 us
  Pallas kernels  34.7 us (94%)
  other arithmetic  1.27 us (3%)
  between operations  0.64 us (2%)
    pallas_call x1, Pallas kernels, local(): pl.pallas_call(functools.partial(kernel, n, zs, ys, cs, own), out_shape=j...  34.7 us
    mul x1, other arithmetic, local(): return (out[0, :own] / variants, 20.0 / variants * out[1, :own])  1.27 us

profile of v3, /device:TPU:0, one launch (start us, length us, event | category | flops | bytes accessed | tf_op | source)
XLA Modules:
  0.0 36.6 jit_solution(10528214564451679940)
XLA Ops:
  0.6 34.7 %shard_map.50 = f32[8,256]{1,0:T(8,128)} custom-call(bf16[16,8192]{1,0:T(8,128)(2,1)} %dose_in.1, f32[16,16]{1,0:T(8,128)} %cov_in.1, f32[16,1792]{1,0:T(8,128)} %pheno_in.1), custom_call_target="tpu_custom_call" | custom-call | tf_op jit(solution)/shard_map/pallas_call | solution.py:335
  35.3 1.3 %multiply_bitcast_fusion = (f32[112]{0:T(128)}, f32[112]{0:T(128)}) fusion(f32[8,256]{1,0:T(8,128)} %shard_map.50), kind=kLoop, calls=%fused_computation | loop fusion | flops 224 | bytes 1792 | tf_op jit(solution)/shard_map/mul | solution.py:359

commit v4 on v3

--- a/solution.py
+++ b/solution.py
@@ -154,6 +154,14 @@
     ).astype(jnp.float32)
     covt = dot(eye, cov, 1, 1)
     solve = dot(cov, inverse(dot(covt, cov, 1, 0)), 1, 0)
+    solve_parts = jnp.concatenate([solve] * 3, axis=1)
+    cov_hi = cov.astype(jnp.bfloat16)
+    cov_rest = cov - cov_hi.astype(jnp.float32)
+    cov_mid = cov_rest.astype(jnp.bfloat16)
+    cov_low = cov_rest - cov_mid.astype(jnp.float32)
+    cov_parts = jnp.concatenate(
+        [cov_hi.astype(jnp.float32), cov_mid.astype(jnp.float32), cov_low], axis=1
+    ).astype(jnp.bfloat16)
 
     def blk_z(o, dev):
         return remote(blocks.at[o], blocks.at[o], z_send.at[dev // (cs * ys)], blk_recv.at[o], dev)
@@ -199,8 +207,9 @@
             src = index(p // cs, lax.rem(y + 1, ys), lax.rem(p, cs))
             dose_copy(src, me).wait_recv()
 
-    dose = dose_all[...].astype(jnp.float32).T
-    dose = dose - dot(dot(dose, cov, 1, 0), solve, 1, 1)
+    dose_bf = dose_all[...].T
+    cov_dose = dot(dose_bf, cov_parts, 1, 0, None)
+    dose = dose_bf.astype(jnp.float32) - dot(cov_dose, solve_parts, 1, 1)
     doset[...] = dose.astype(jnp.bfloat16)
     dose_var = jnp.sum(dose * dose, axis=1, keepdims=True) / samples + 0.1
     scale[...] = jnp.broadcast_to(1.0 / (samples * dose_var), scale.shape)

time: 37.1 us -> 35.2 us (0.949)
  Pallas kernels: 34.7 us -> 33 us
    pallas_call x1, Pallas kernels: 34.7 us -> 33 us  [local(): pl.pallas_call(functools.partial(kernel, n, zs, ys, cs, own), out_shape=j...]
where the time goes in v4:
time: 35.2 us; the launch traced here: 34.9 us
  Pallas kernels  33 us (94%)
  other arithmetic  1.27 us (4%)
  between operations  0.64 us (2%)
    pallas_call x1, Pallas kernels, local(): pl.pallas_call(functools.partial(kernel, n, zs, ys, cs, own), out_shape=j...  33 us
    mul x1, other arithmetic, local(): return (out[0, :own] / variants, 20.0 / variants * out[1, :own])  1.27 us

profile of v4, /device:TPU:0, one launch (start us, length us, event | category | flops | bytes accessed | tf_op | source)
XLA Modules:
  0.0 34.9 jit_solution(15450134020562881836)
XLA Ops:
  0.6 33.0 %shard_map.50 = f32[8,256]{1,0:T(8,128)} custom-call(bf16[16,8192]{1,0:T(8,128)(2,1)} %dose_in.1, f32[16,16]{1,0:T(8,128)} %cov_in.1, f32[16,1792]{1,0:T(8,128)} %pheno_in.1), custom_call_target="tpu_custom_call" | custom-call | tf_op jit(solution)/shard_map/pallas_call | solution.py:344
  33.6 1.3 %multiply_bitcast_fusion = (f32[112]{0:T(128)}, f32[112]{0:T(128)}) fusion(f32[8,256]{1,0:T(8,128)} %shard_map.50), kind=kLoop, calls=%fused_computation | loop fusion | flops 224 | bytes 1792 | tf_op jit(solution)/shard_map/mul | solution.py:368

commit v5 on v4

--- a/solution.py
+++ b/solution.py
@@ -29,6 +29,16 @@
         row = work[k : k + 1, :] / work[k : k + 1, k : k + 1]
         work = jnp.where(row_id == k, row, work - work[:, k : k + 1] * row)
     return work[:, size:]
+
+
+def partner(a, k, count):
+    if count & (count - 1):
+        return lax.rem(a + k, count)
+    out, bit = 0, 1
+    while bit < count:
+        out = out + lax.rem(a // bit + k // bit, 2) * bit
+        bit *= 2
+    return out
 
 
 def kernel(
@@ -112,7 +122,7 @@
     def others(body):
         @pl.loop(1, n)
         def _(k):
-            body(lax.rem(me + k, n))
+            body(partner(me, k, n))
 
     others(lambda dev: cov_copy(me, dev).start())
 
@@ -124,7 +134,7 @@
     def group(body):
         @pl.loop(1, peers)
         def _(k):
-            body(at_place(lax.rem(place + k, peers)))
+            body(at_place(partner(place, k, peers)))
 
     y_dev = index(z, lax.rem(y + 1, ys), c)
     c_dev = index(z, y, lax.rem(c + 1, cs))
@@ -190,7 +200,7 @@
         blocks[place, pl.ds(samples, 16), :] = extra.astype(jnp.bfloat16)
         blocks[place, pl.ds(0, samples), :] = resid.astype(jnp.bfloat16)
         for k in range(1, zs):
-            blk_z(place, index(lax.rem(z + k, zs), y, c)).start()
+            blk_z(place, index(partner(z, k, zs), y, c)).start()
         if cs > 1:
             blk_c(place, c_dev).start()
 
@@ -203,7 +213,7 @@
     if ys > 1:
         @pl.loop(0, peers)
         def _(k):
-            p = lax.rem(place + k, peers)
+            p = partner(place, k, peers)
             src = index(p // cs, lax.rem(y + 1, ys), lax.rem(p, cs))
             dose_copy(src, me).wait_recv()
 
@@ -230,7 +240,7 @@
 
     @pl.loop(1, zs)
     def _(k):
-        o = lax.rem(z + k, zs) * cs + c
+        o = partner(z, k, zs) * cs + c
 
         @pl.when(o < nb)
         def _():
@@ -242,7 +252,7 @@
     if cs > 1:
         @pl.loop(0, zs)
         def _(k):
-            o = lax.rem(z + k, zs) * cs + lax.rem(c + 1, cs)
+            o = partner(z, k, zs) * cs + lax.rem(c + 1, cs)
 
             @pl.when(o < nb)
             def _():
@@ -252,7 +262,7 @@
     window = landed.shape[2]
 
     def owner(k):
-        return y * peers + lax.rem(place + k, peers)
+        return y * peers + partner(place, k, peers)
 
     def first(dev):
         return jnp.minimum(own * lax.rem(dev, peers) // LANES * LANES, nb * LANES - window)
@@ -314,12 +324,12 @@
     @pl.when(place < nb)
     def _():
         for k in range(1, zs):
-            blk_z(place, index(lax.rem(z + k, zs), y, c)).wait_send()
+            blk_z(place, index(partner(z, k, zs), y, c)).wait_send()
 
     if cs > 1:
         @pl.loop(0, zs)
         def _(k):
-            o = lax.rem(z + k, zs) * cs + c
+            o = partner(z, k, zs) * cs + c
 
             @pl.when(o < nb)
             def _():
@@ -343,7 +353,7 @@
     dma = pltpu.SemaphoreType.DMA
     out = pl.pallas_call(
         functools.partial(kernel, n, zs, ys, cs, own),
-        out_shape=jax.ShapeDtypeStruct((8, window), jnp.float32),
+        out_shape=jax.ShapeDtypeStruct((2, window), jnp.float32),
         in_specs=[pl.BlockSpec(memory_space=pl.ANY)] * 3,
         out_specs=pl.BlockSpec(memory_space=pltpu.VMEM),
         scratch_shapes=[
@@ -357,8 +367,8 @@
             pltpu.VMEM((nb, samples + 16, LANES), jnp.bfloat16),
             pltpu.VMEM((width, samples), jnp.bfloat16),
             pltpu.VMEM((width, LANES), jnp.float32),
-            pltpu.VMEM((8, nb * LANES), jnp.float32),
-            pltpu.VMEM((peers, 8, window), jnp.float32),
+            pltpu.VMEM((2, nb * LANES), jnp.float32),
+            pltpu.VMEM((peers, 2, window), jnp.float32),
             pltpu.VMEM((8, LANES), jnp.float32),
             dma((n,)), dma((n,)), dma((n,)), dma((n,)), dma((n,)), dma((n,)),
             dma((zs,)), dma((n,)), dma((nb,)), dma((nb,)), dma((peers,)), dma((peers,)),

time: 35.2 us -> 33.4 us (0.949)
  Pallas kernels: 33 us -> 31.3 us
    pallas_call x1, Pallas kernels: 33 us -> 31.3 us  [local(): pl.pallas_call(functools.partial(kernel, n, zs, ys, cs, own), out_shape=j...]
where the time goes in v5:
time: 33.4 us; the launch traced here: 33.2 us
  Pallas kernels  31.3 us (94%)
  other arithmetic  1.25 us (4%)
  between operations  0.64 us (2%)
    pallas_call x1, Pallas kernels, local(): pl.pallas_call(functools.partial(kernel, n, zs, ys, cs, own), out_shape=j...  31.3 us
    mul x1, other arithmetic, local(): return (out[0, :own] / variants, 20.0 / variants * out[1, :own])  1.25 us

profile of v5, /device:TPU:0, one launch (start us, length us, event | category | flops | bytes accessed | tf_op | source)
XLA Modules:
  0.0 33.2 jit_solution(5995702155786302975)
XLA Ops:
  0.6 31.3 %shard_map.50 = f32[2,256]{1,0:T(2,128)} custom-call(bf16[16,8192]{1,0:T(8,128)(2,1)} %dose_in.1, f32[16,16]{1,0:T(8,128)} %cov_in.1, f32[16,1792]{1,0:T(8,128)} %pheno_in.1), custom_call_target="tpu_custom_call" | custom-call | tf_op jit(solution)/shard_map/pallas_call | solution.py:354
  31.9 1.3 %multiply_bitcast_fusion = (f32[112]{0:T(128)}, f32[112]{0:T(128)}) fusion(f32[2,256]{1,0:T(2,128)} %shard_map.50), kind=kLoop, calls=%fused_computation | loop fusion | flops 224 | bytes 1792 | tf_op jit(solution)/shard_map/mul | solution.py:378
